TPU v7x, 32 devices: a whole 2x2x4 slice. The times are simulated.
32 devices in a mesh: unit: 2 (over y), row: 4 (over x, core), col: 4 (over z).
Axes of the slice: x: 2, y: 2, z: 4, core: 2. Of those that a mesh axis runs over, the one named last changes fastest.
Arguments:
- tracer: float32 [4, 32, 64, 64], P('unit', None, 'row', 'col'), parts along dimension 0, may hold values from -6 to 6
- symbol_x: float32 [32], replicated, may hold values from 0.3 to 3
- symbol_y: float32 [64], replicated, may hold values from 0.3 to 3
- symbol_z: float32 [64], replicated, may hold values from 0.3 to 3
Outputs:
- smoothed: float32 [4, 32, 64, 64], P('unit', None, 'row', 'col'), parts along dimension 0
There are 2 independent parts, one for each index of `unit`. A program takes and returns all parts, laid end to end along the dimension named above; an argument that names none is the same for every part. Nothing has to cross between parts.
All inputs are finite; a program needn't handle non-finite values.
Results may differ from a plain program's by a relative error of at most 0.0003.
Values sent between devices are 32-bit elements.
A program may use at most 64 MiB of HBM per device.

v0:
```python
import jax
import jax.numpy as jnp
from jax import lax
from jax.sharding import PartitionSpec as P


def mode_table(count):
    rank = jnp.arange(count)
    angle = (
        jnp.pi
        / (4 * count)
        * ((2 * rank[:, None] + 1) * (2 * rank[None, :] + 1) % (8 * count)).astype(jnp.float32)
    )
    return jnp.cos(angle) * (2.0 / count) ** 0.5


def to_modes(values, dim):
    moved = jnp.tensordot(
        values, mode_table(values.shape[dim]), axes=([dim], [0]), precision=lax.Precision.HIGHEST
    )
    return jnp.moveaxis(moved, -1, dim)


def shards(tracer, symbol_x, symbol_y, symbol_z):

    def forward_part(part_values):
        part_values = to_modes(part_values, 1)
        part_values = lax.all_to_all(part_values, "row", split_axis=1, concat_axis=2, tiled=True)
        part_values = to_modes(part_values, 2)
        part_values = lax.all_to_all(part_values, "col", split_axis=2, concat_axis=3, tiled=True)
        return to_modes(part_values, 3)

    def backward_part(part_values):
        part_values = to_modes(part_values, 3)
        part_values = lax.all_to_all(part_values, "col", split_axis=3, concat_axis=2, tiled=True)
        part_values = to_modes(part_values, 2)
        part_values = lax.all_to_all(part_values, "row", split_axis=2, concat_axis=1, tiled=True)
        return to_modes(part_values, 1)

    block_values = forward_part(tracer)
    share_x = block_values.shape[1]
    part_x = lax.dynamic_slice_in_dim(symbol_x, lax.axis_index("row") * share_x, share_x)
    share_y = block_values.shape[2]
    part_y = lax.dynamic_slice_in_dim(symbol_y, lax.axis_index("col") * share_y, share_y)
    symbol = part_x[:, None, None] + part_y[None, :, None] + symbol_z[None, None, :]
    block_values = block_values * lax.rsqrt(symbol)
    block_values = backward_part(block_values)
    return block_values


def solution(mesh):
    in_specs = (P("unit", None, "row", "col"), P(), P(), P())
    out_specs = P("unit", None, "row", "col")
    return jax.shard_map(shards, mesh=mesh, in_specs=in_specs, out_specs=out_specs, check_vma=False)
```

profile of v0, /device:TPU:0, one launch (start us, length us, event | category | flops | bytes accessed | tf_op | source)
XLA Modules:
  0.0 49.6 jit_solution(17201556135171199942)
XLA Ops:
  0.0 0.0 copy-start
  0.0 0.9 %copy-done = f32[2,32,16,16]{1,3,2,0:T(8,128)S(1)} copy-done((f32[2,32,16,16]{1,3,2,0:T(8,128)S(1)}, f32[2,32,16,16]{1,3,2,0:T(8,128)}, u32[]{:S(2)}) %copy-start) | copy-done | bytes 65560
  1.0 0.5 %fusion.47 = f32[32,512]{0,1:S(1)} fusion(f32[32,512]{0,1:T(8,128)S(1)} %bitcast.57, s32[32]{0:T(128)S(1)} %multiply_add_fusion.1), kind=kOutput, calls=%fused_computation.59 | convolution fusion | flops 6306816 | bytes 131200
  1.5 0.5 copy.14
  1.9 0.9 %reshape.67 = f32[4,1,4096]{2,1,0:T(1,128)} reshape(f32[32,2,16,16]{3,2,1,0:T(8,128)S(1)} %bitcast.61) | data formatting | bytes 131072
  2.8 4.3 %all-to-all-start = ((f32[4,1,4096]{2,1,0:T(1,128)}), f32[4,1,4096]{2,1,0:T(1,128)S(1)}, u32[]{:S(2)}, u32[]{:S(2)}) async-start(f32[4,1,4096]{2,1,0:T(1,128)} %reshape.67), calls=%async_computation | async-start | bytes 131072 | tf_op jit(solution)/shard_map/all_to_all | solution.py:28
  7.1 0.0 copy-start.2
  7.1 0.7 %copy-done.2 = f32[64]{0:T(128)S(1)} copy-done((f32[64]{0:T(128)S(1)}, f32[64]{0:T(128)}, u32[]{:S(2)}) %copy-start.2) | copy-done | bytes 280
  7.7 0.1 dynamic_slice.7
  7.8 0.0 copy-start.3
  7.8 0.7 %copy-done.3 = f32[32]{0:T(128)S(1)} copy-done((f32[32]{0:T(128)S(1)}, f32[32]{0:T(128)}, u32[]{:S(2)}) %copy-start.3) | copy-done | bytes 152
  8.5 0.1 dynamic_slice.6
  8.5 0.1 broadcast_add_fusion
  8.6 2.6 %all-to-all-done = f32[4,1,4096]{2,1,0:T(1,128)S(1)} async-done(((f32[4,1,4096]{2,1,0:T(1,128)}), f32[4,1,4096]{2,1,0:T(1,128)S(1)}, u32[]{:S(2)}, u32[]{:S(2)}) %all-to-all-start) | async-done | bytes 65568 | tf_op jit(solution)/shard_map/all_to_all | solution.py:28
  11.2 0.6 %broadcast.193 = f32[]{:T(128)} broadcast(f32[]{:T(128)} %constant.155), dimensions={} | broadcast | bytes 8 | tf_op jit(solution)/shard_map/all_to_all | solution.py:28
  11.8 0.9 %reduce = f32[4,4096]{1,0:T(4,128)S(1)} reduce(f32[4,1,4096]{2,1,0:T(1,128)S(1)} %all-to-all-done, f32[]{:T(128)} %broadcast.193), dimensions={1}, to_apply=%all_to_all.52.reduce_sub_computation | reduce | bytes 131076 | tf_op jit(solution)/shard_map/all_to_all | solution.py:28
  12.6 0.2 reshape.68
  12.9 0.2 copy.16
  13.1 0.3 all_to_all.55
  13.4 0.5 convolution_bitcast_fusion.2
  13.8 0.3 copy.17
  14.1 0.9 %reshape.69 = f32[4,1,4096]{2,1,0:T(1,128)} reshape(f32[64,2,8,16]{3,2,1,0:T(8,128)S(1)} %bitcast.58) | data formatting | bytes 131072
  15.0 0.0 copy-start.1
  15.0 5.5 %all-to-all-start.1 = ((f32[4,1,4096]{2,1,0:T(1,128)}), f32[4,1,4096]{2,1,0:T(1,128)S(1)}, u32[]{:S(2)}, u32[]{:S(2)}) async-start(f32[4,1,4096]{2,1,0:T(1,128)} %reshape.69), calls=%async_computation.1 | async-start | bytes 131072 | tf_op jit(solution)/shard_map/all_to_all | solution.py:30
  20.5 0.0 copy-done.1
  20.5 0.1 add_rsqrt_fusion
  20.6 5.6 %all-to-all-done.1 = f32[4,1,4096]{2,1,0:T(1,128)S(1)} async-done(((f32[4,1,4096]{2,1,0:T(1,128)}), f32[4,1,4096]{2,1,0:T(1,128)S(1)}, u32[]{:S(2)}, u32[]{:S(2)}) %all-to-all-start.1) | async-done | bytes 65568 | tf_op jit(solution)/shard_map/all_to_all | solution.py:30
  26.2 0.9 %reduce.1 = f32[4,4096]{1,0:T(4,128)S(1)} reduce(f32[4,1,4096]{2,1,0:T(1,128)S(1)} %all-to-all-done.1, f32[]{:T(128)} %broadcast.193), dimensions={1}, to_apply=%all_to_all.56.reduce_sub_computation | reduce | bytes 131076 | tf_op jit(solution)/shard_map/all_to_all | solution.py:30
  27.1 0.2 reshape.70
  27.3 0.3 copy.32
  27.6 0.3 all_to_all.59
  27.9 0.5 convolution_multiply_fusion
  28.3 0.5 fusion.8
  28.8 0.3 copy.19
  29.1 0.2 reshape.71
  29.3 8.1 %all_to_all.72 = f32[4,1,4096]{2,1,0:T(1,128)S(1)} all-to-all(f32[4,1,4096]{2,1,0:T(1,128)S(1)} %reshape.71), channel_id=1, replica_groups=mesh['unit'=2,'row'=4,'col'=4] {'col'}, dimensions={0} | all-to-all | bytes 131072 | tf_op jit(solution)/shard_map/all_to_all | solution.py:35
  37.4 0.9 %reduce.2 = f32[4,4096]{1,0:T(4,128)S(1)} reduce(f32[4,1,4096]{2,1,0:T(1,128)S(1)} %all_to_all.72, f32[]{:T(128)} %broadcast.193), dimensions={1}, to_apply=%all_to_all.60.reduce_sub_computation | reduce | bytes 131076 | tf_op jit(solution)/shard_map/all_to_all | solution.py:35
  38.3 0.2 reshape.72
  38.5 0.3 copy.31
  38.8 0.3 all_to_all.63
  39.1 0.4 convolution_bitcast_fusion.1
  39.6 0.3 copy.21
  39.8 0.2 reshape.73
  40.1 6.5 %all_to_all.73 = f32[4,1,4096]{2,1,0:T(1,128)S(1)} all-to-all(f32[4,1,4096]{2,1,0:T(1,128)S(1)} %reshape.73), channel_id=1, replica_groups=mesh['unit'=2,'row'=4,'col'=4] {'row'}, dimensions={0} | all-to-all | bytes 131072 | tf_op jit(solution)/shard_map/all_to_all | solution.py:37
  46.6 0.9 %reduce.3 = f32[4,4096]{1,0:T(4,128)S(1)} reduce(f32[4,1,4096]{2,1,0:T(1,128)S(1)} %all_to_all.73, f32[]{:T(128)} %broadcast.193), dimensions={1}, to_apply=%all_to_all.64.reduce_sub_computation | reduce | bytes 131076 | tf_op jit(solution)/shard_map/all_to_all | solution.py:37
  47.4 0.2 reshape.74
  47.6 0.2 copy.22
  47.8 1.8 %convolution_bitcast_fusion = f32[2,32,16,16]{1,3,2,0:T(8,128)} fusion(f32[2,32,16,16]{3,2,1,0:T(8,128)S(1)} %bitcast.64, s32[32]{0:T(128)S(1)} %multiply_add_fusion.1), kind=kOutput, calls=%fused_computation | convolution fusion | flops 6306816 | bytes 131200 | tf_op jit(solution)/shard_map/dot_general | solution.py:18
  (2 shorter events, 0.0 us)
Async XLA Ops:
  0.0 1.0 %copy-start = (f32[2,32,16,16]{1,3,2,0:T(8,128)S(1)}, f32[2,32,16,16]{1,3,2,0:T(8,128)}, u32[]{:S(2)}) copy-start(f32[2,32,16,16]{1,3,2,0:T(8,128)} %param.4) | copy-start | bytes 196612
  2.8 8.4 %all-to-all-start = ((f32[4,1,4096]{2,1,0:T(1,128)}), f32[4,1,4096]{2,1,0:T(1,128)S(1)}, u32[]{:S(2)}, u32[]{:S(2)}) async-start(f32[4,1,4096]{2,1,0:T(1,128)} %reshape.67), calls=%async_computation | async-start | bytes 131072 | tf_op jit(solution)/shard_map/all_to_all | solution.py:28
  7.1 0.7 %copy-start.2 = (f32[64]{0:T(128)S(1)}, f32[64]{0:T(128)}, u32[]{:S(2)}) copy-start(f32[64]{0:T(128)} %param.6) | copy-start | bytes 772
  7.8 0.7 %copy-start.3 = (f32[32]{0:T(128)S(1)}, f32[32]{0:T(128)}, u32[]{:S(2)}) copy-start(f32[32]{0:T(128)} %param.5) | copy-start | bytes 388
  15.0 5.5 %copy-start.1 = (f32[64]{0:T(128)S(1)}, f32[64]{0:T(128)}, u32[]{:S(2)}) copy-start(f32[64]{0:T(128)} %param.7) | copy-start | bytes 772
  15.0 11.2 %all-to-all-start.1 = ((f32[4,1,4096]{2,1,0:T(1,128)}), f32[4,1,4096]{2,1,0:T(1,128)S(1)}, u32[]{:S(2)}, u32[]{:S(2)}) async-start(f32[4,1,4096]{2,1,0:T(1,128)} %reshape.69), calls=%async_computation.1 | async-start | bytes 131072 | tf_op jit(solution)/shard_map/all_to_all | solution.py:30
where the time goes:
time: 50.1 us; the launch traced here: 49.6 us
  blocking collectives  14.6 us (29%)
  starting transfers between devices  9.76 us (19%)
  local copies, waits for them, and re-layouts  9.15 us (18%)
  waiting for transfers between devices  8.23 us (16%)
  matrix products  4.09 us (8%)
  other arithmetic  3.59 us (7%)
    all_to_all x1, blocking collectives, backward_part(): lax.all_to_all(part_values, 'col', split_axis=3, concat_axis=2, tiled=True)  8.11 us
    all_to_all x1, blocking collectives, backward_part(): lax.all_to_all(part_values, 'row', split_axis=2, concat_axis=1, tiled=True)  6.49 us
    all_to_all x1, waiting for transfers between devices, forward_part(): lax.all_to_all(part_values, 'col', split_axis=2, concat_axis=3, tiled=True)  5.65 us
    all_to_all x1, starting transfers between devices, forward_part(): lax.all_to_all(part_values, 'col', split_axis=2, concat_axis=3, tiled=True)  5.49 us
    unnamed x16, local copies, waits for them, and re-layouts  5.27 us
    all_to_all x1, starting transfers between devices, forward_part(): lax.all_to_all(part_values, 'row', split_axis=1, concat_axis=2, tiled=True)  4.27 us
    dot_general x5, matrix products, to_modes(): jnp.tensordot(values, mode_table(values.shape[dim]), axes=([dim], [0]), p...  3.59 us
    all_to_all x1, waiting for transfers between devices, forward_part(): lax.all_to_all(part_values, 'row', split_axis=1, concat_axis=2, tiled=True)  2.58 us
  transfers between devices with their start and end apart: 2, of which 2 were waited for; matrix products, arithmetic and copies ran while one was open for 1% of the time, Pallas kernels for 0%

commit v1 on v0

v1 whole, which is shorter than its diff:
```python
import functools

import jax
import jax.numpy as jnp
import numpy as np
from jax import lax
from jax.experimental import pallas as pl
from jax.experimental.pallas import tpu as pltpu
from jax.sharding import PartitionSpec as P

MESH = pl.DeviceIdType.MESH
LANES = 128
ROWS = 8


def mode_table(count):
    rank = np.arange(count)
    angle = np.pi / (4 * count) * ((2 * rank[:, None] + 1) * (2 * rank[None, :] + 1) % (8 * count))
    return np.cos(angle) * (2.0 / count) ** 0.5


def two_parts(table):
    high = table.astype(jnp.bfloat16)
    low = (table - high.astype(np.float64)).astype(jnp.bfloat16)
    return np.stack([high, low])


def split(values):
    high = values.astype(jnp.bfloat16)
    return high, (values - high.astype(jnp.float32)).astype(jnp.bfloat16)


def dot(a, b):
    return jnp.dot(a, b, preferred_element_type=jnp.float32)


def right(values, table):
    rows = values.shape[0]
    high, low = split(values)
    both = dot(jnp.concatenate([high, low], axis=0), table[0])
    return both[:rows] + (both[rows:] + dot(high, table[1]))


def left(table, values):
    high, low = split(values)
    return dot(table, jnp.concatenate([high, high, low], axis=0))


def swap_blocks(tiles):
    count = len(tiles)
    block = LANES // count
    which = lax.broadcasted_iota(jnp.int32, tiles[0].shape, 1) // block
    out = []
    for j in range(count):
        tile = tiles[j]
        for i in range(count):
            if i != j:
                moved = pltpu.roll(tiles[i], ((i - j) * block) % LANES, 1)
                tile = jnp.where(which == i, moved, tile)
        out.append(tile)
    return out


def kernel(
    sizes, x_ref, sx_ref, sy_ref, sz_ref, wx_ref, wxt_ref, wy_ref, hz_ref, out_ref,
    send, recv, send_back, recv_back, send_sem, recv_sem, send_back_sem, recv_back_sem,
):
    fields, count_x, rows_n, cols_n, share_y, share_z, planes = sizes
    devices = rows_n * cols_n
    me = lax.axis_index("row") * cols_n + lax.axis_index("col")
    high_y, high_z = share_y // ROWS, share_z // ROWS
    groups = count_x // planes

    def place(index):
        return {"row": index // cols_n, "col": index % cols_n}

    barrier = pltpu.get_barrier_semaphore()
    for step in range(1, devices):
        peer = lax.rem(me + step, devices)
        pl.semaphore_signal(barrier, inc=1, device_id=place(peer), device_id_type=MESH)

    def exchange(source, target, source_sem, target_sem):
        copies = []
        for step in range(1, devices):
            peer = lax.rem(me + step, devices)
            copy = pltpu.make_async_remote_copy(
                src_ref=source.at[peer],
                dst_ref=target.at[me],
                send_sem=source_sem.at[peer],
                recv_sem=target_sem.at[me],
                device_id=place(peer),
                device_id_type=MESH,
            )
            copy.start()
            copies.append(copy)
        target[me] = source[me]
        return copies

    def arrive(copies, source, target, target_sem):
        for step in range(1, devices):
            peer = lax.rem(me + step, devices)
            pltpu.make_async_remote_copy(
                src_ref=source.at[peer],
                dst_ref=target.at[peer],
                send_sem=target_sem.at[peer],
                recv_sem=target_sem.at[peer],
                device_id=place(peer),
                device_id_type=MESH,
            ).wait_recv()

    packed = jnp.concatenate(
        [
            jnp.concatenate([x_ref[f * share_y + h * ROWS + y] for y in range(ROWS)], axis=1)
            for f in range(fields)
            for h in range(high_y)
        ],
        axis=0,
    )
    modes = right(packed, wx_ref)
    lane_tiles = count_x * ROWS // LANES
    per_tile = groups // lane_tiles

    def at(f, h, z, t):
        row = ((f * high_y + h) * high_z + z) * ROWS
        return modes[row : row + ROWS, t * LANES : (t + 1) * LANES]

    for f in range(fields):
        for t in range(lane_tiles):
            tiles = [at(f, h, z, t) for z in range(high_z) for h in range(high_y)]
            for i, tile in enumerate(swap_blocks(tiles)):
                send[f * groups + t * per_tile + i] = tile

    pl.semaphore_wait(barrier, devices - 1)
    copies = exchange(send, recv, send_sem, recv_sem)

    count_z, count_y = sz_ref.shape[1], sy_ref.shape[1]
    width = rows_n * high_y * planes * ROWS

    def column(row, size):
        diagonal = lax.broadcasted_iota(jnp.int32, (size, size), 0) == lax.broadcasted_iota(
            jnp.int32, (size, size), 1
        )
        return jnp.sum(jnp.where(diagonal, row, 0.0), axis=1, keepdims=True)

    symbol_z = column(sz_ref[...], count_z)
    lane = lax.broadcasted_iota(jnp.int32, (count_y, width), 1)
    rank = lane // (planes * ROWS) * ROWS + lane % ROWS
    chosen = rank == lax.broadcasted_iota(jnp.int32, (count_y, width), 0)
    symbol = jnp.sum(
        jnp.where(chosen, column(sy_ref[...], count_y), 0.0), axis=0, keepdims=True
    )
    plane = lax.broadcasted_iota(jnp.int32, (1, width), 1) // ROWS % planes
    first = lax.rem(me, groups) * planes
    symbol_x = jnp.zeros((1, width), jnp.float32)
    for p in range(planes):
        symbol_x = jnp.where(plane == p, sx_ref[first + p], symbol_x)
    factor = lax.rsqrt(symbol_x + symbol + symbol_z)

    arrive(copies, send, recv, recv_sem)

    lane_tiles = width // LANES
    grid = [[None] * lane_tiles for _ in range(cols_n * high_z)]
    for c in range(cols_n):
        for t in range(lane_tiles):
            tiles = [recv[(t * high_z + i) * cols_n + c] for i in range(high_z)]
            for z, tile in enumerate(swap_blocks(tiles)):
                grid[c * high_z + z][t] = tile
    block = jnp.concatenate([jnp.concatenate(row, axis=1) for row in grid], axis=0)
    block = right(block, wy_ref)
    block = left(hz_ref[...], block)
    block = block * factor
    block = left(hz_ref[...], block)
    block = right(block, wy_ref)
    for c in range(cols_n):
        for t in range(lane_tiles):
            tiles = [
                block[
                    (c * high_z + z) * ROWS : (c * high_z + z + 1) * ROWS,
                    t * LANES : (t + 1) * LANES,
                ]
                for z in range(high_z)
            ]
            for i, tile in enumerate(swap_blocks(tiles)):
                send_back[(t * high_z + i) * cols_n + c] = tile

    back_copies = exchange(send_back, recv_back, send_back_sem, recv_back_sem)
    for copy in copies:
        copy.wait_send()
    arrive(back_copies, send_back, recv_back, recv_back_sem)

    lane_tiles = count_x * ROWS // LANES
    grid = [[None] * lane_tiles for _ in range(fields * high_y * high_z)]
    for f in range(fields):
        for t in range(lane_tiles):
            tiles = [recv_back[f * groups + t * per_tile + i] for i in range(per_tile)]
            for i, tile in enumerate(swap_blocks(tiles)):
                z, h = divmod(i, high_y)
                grid[(f * high_y + h) * high_z + z][t] = tile
    modes = jnp.concatenate([jnp.concatenate(row, axis=1) for row in grid], axis=0)
    values = right(modes, wxt_ref)
    for f in range(fields):
        for h in range(high_y):
            row = (f * high_y + h) * share_z
            for y in range(ROWS):
                out_ref[f * share_y + h * ROWS + y] = values[
                    row : row + share_z, y * count_x : (y + 1) * count_x
                ]
    for copy in back_copies:
        copy.wait_send()


def fused(sizes, tracer, symbol_x, symbol_y, symbol_z):
    fields, count_x, rows_n, cols_n, share_y, share_z, planes = sizes
    devices = rows_n * cols_n
    count_y, count_z = symbol_y.shape[0], symbol_z.shape[0]
    high_y = share_y // ROWS

    table_x = np.einsum("xk,ab->axkb", mode_table(count_x), np.eye(ROWS))
    table_x = table_x.reshape(ROWS * count_x, count_x * ROWS)
    blocks = rows_n * high_y
    table_y = np.einsum(
        "aybz,kl->akyblz",
        mode_table(count_y).reshape(blocks, ROWS, blocks, ROWS),
        np.eye(planes),
    ).reshape(blocks * planes * ROWS, blocks * planes * ROWS)
    high, low = two_parts(mode_table(count_z))
    table_z = np.concatenate([high, low, high], axis=1)

    values = jnp.transpose(tracer, (0, 2, 3, 1)).reshape(fields * share_y, share_z, count_x)
    vmem = pl.BlockSpec(memory_space=pltpu.VMEM)
    smem = pl.BlockSpec(memory_space=pltpu.SMEM)
    tile = pltpu.VMEM((devices, ROWS, LANES), jnp.float32)
    out = pl.pallas_call(
        functools.partial(kernel, sizes),
        out_shape=jax.ShapeDtypeStruct(values.shape, jnp.float32),
        in_specs=[vmem, smem] + [vmem] * 6,
        out_specs=vmem,
        scratch_shapes=[tile] * 4 + [pltpu.SemaphoreType.DMA((devices,))] * 4,
        compiler_params=pltpu.CompilerParams(collective_id=0, has_side_effects=True),
    )(
        values,
        symbol_x,
        symbol_y.reshape(1, -1),
        symbol_z.reshape(1, -1),
        jnp.asarray(two_parts(table_x)),
        jnp.asarray(two_parts(table_x.T)),
        jnp.asarray(two_parts(table_y)),
        jnp.asarray(table_z),
    )
    out = out.reshape(fields, share_y, share_z, count_x)
    return jnp.transpose(out, (0, 3, 1, 2))


def to_modes(values, dim):
    table = jnp.asarray(mode_table(values.shape[dim]), jnp.float32)
    moved = jnp.tensordot(values, table, axes=([dim], [0]), precision=lax.Precision.HIGHEST)
    return jnp.moveaxis(moved, -1, dim)


def by_lines(values, symbol_x, symbol_y, symbol_z):
    values = to_modes(values, 1)
    values = lax.all_to_all(values, "row", split_axis=1, concat_axis=2, tiled=True)
    values = to_modes(values, 2)
    values = lax.all_to_all(values, "col", split_axis=2, concat_axis=3, tiled=True)
    values = to_modes(values, 3)
    share_x, share_y = values.shape[1], values.shape[2]
    part_x = lax.dynamic_slice_in_dim(symbol_x, lax.axis_index("row") * share_x, share_x)
    part_y = lax.dynamic_slice_in_dim(symbol_y, lax.axis_index("col") * share_y, share_y)
    symbol = part_x[:, None, None] + part_y[None, :, None] + symbol_z[None, None, :]
    values = values * lax.rsqrt(symbol)
    values = to_modes(values, 3)
    values = lax.all_to_all(values, "col", split_axis=3, concat_axis=2, tiled=True)
    values = to_modes(values, 2)
    values = lax.all_to_all(values, "row", split_axis=2, concat_axis=1, tiled=True)
    return to_modes(values, 1)


def solution(mesh):
    rows_n, cols_n = mesh.shape["row"], mesh.shape["col"]

    def shards(tracer, symbol_x, symbol_y, symbol_z):
        fields, count_x, share_y, share_z = tracer.shape
        planes = fields * count_x // (rows_n * cols_n)
        high_y, high_z = share_y // ROWS, share_z // ROWS
        whole_tiles = (
            planes * rows_n * cols_n == fields * count_x
            and count_x % planes == 0
            and high_y * ROWS == share_y
            and high_z * ROWS == share_z
            and planes * ROWS * high_y * high_z == LANES
            and count_x * ROWS % LANES == 0
            and rows_n % high_z == 0
        )
        if not whole_tiles:
            return by_lines(tracer, symbol_x, symbol_y, symbol_z)
        sizes = fields, count_x, rows_n, cols_n, share_y, share_z, planes
        return fused(sizes, tracer, symbol_x, symbol_y, symbol_z)

    in_specs = (P("unit", None, "row", "col"), P(), P(), P())
    out_specs = P("unit", None, "row", "col")
    return jax.shard_map(shards, mesh=mesh, in_specs=in_specs, out_specs=out_specs, check_vma=False)
```

time: 50.1 us -> 20 us (0.40)
  Pallas kernels: 0 us -> 18.2 us
  blocking collectives: 14.6 us -> 0 us
  starting transfers between devices: 9.76 us -> 0 us
  waiting for transfers between devices: 8.23 us -> 0 us
  local copies, waits for them, and re-layouts: 9.15 us -> 1.67 us
  matrix products: 4.09 us -> 0 us
  other arithmetic: 3.59 us -> 0 us
    pallas_call x0 -> x1, Pallas kernels: none -> 18.2 us  [fused(): pl.pallas_call(functools.partial(kernel, sizes), out_shape=jax.ShapeDtype...]
    all_to_all x2 -> x0, blocking collectives: 14.6 us -> none  [the longest x1 8.11 us: backward_part(): lax.all_to_all(part_values, 'col', split_axis=3, concat_axis=2, tiled=True)]
    all_to_all x2 -> x0, starting transfers between devices: 9.76 us -> none  [the longest x1 5.49 us: forward_part(): lax.all_to_all(part_values, 'col', split_axis=2, concat_axis=3, tiled=True)]
    all_to_all x2 -> x0, waiting for transfers between devices: 8.23 us -> none  [the longest x1 5.65 us: forward_part(): lax.all_to_all(part_values, 'col', split_axis=2, concat_axis=3, tiled=True)]
    unnamed x16 -> x1, local copies, waits for them, and re-layouts: 5.27 us -> 1.67 us
    dot_general x5 -> x0, matrix products: 3.59 us -> none  [to_modes(): jnp.tensordot(values, mode_table(values.shape[dim]), axes=([dim], [0]), p...]
    all_to_all x4 -> x0, other arithmetic: 3.42 us -> none  [the longest x1 0.86 us: backward_part(): lax.all_to_all(part_values, 'row', split_axis=2, concat_axis=1, tiled=True)]
    all_to_all x8 -> x0, local copies, waits for them, and re-layouts: 2.44 us -> none  [the longest x3 1.07 us: forward_part(): lax.all_to_all(part_values, 'row', split_axis=1, concat_axis=2, tiled=True)]
  transfers between devices with their start and end apart: 2 -> 0, of which waited for: 2 -> 0; matrix products, arithmetic and copies ran while one was open for 1% -> 0% of each run, Pallas kernels for 0% -> 0%
where the time goes in v1:
time: 20 us; the launch traced here: 19.9 us
  Pallas kernels  18.2 us (91%)
  local copies, waits for them, and re-layouts  1.67 us (8%)
    pallas_call x1, Pallas kernels, fused(): pl.pallas_call(functools.partial(kernel, sizes), out_shape=jax.ShapeDtype...  18.2 us
    unnamed x1, local copies, waits for them, and re-layouts  1.67 us

profile of v1, /device:TPU:0, one launch (start us, length us, event | category | flops | bytes accessed | tf_op | source)
XLA Modules:
  0.0 19.9 jit_solution(2372505733107765640)
XLA Ops:
  0.0 18.2 %shard_map.82 = f32[32,16,32]{2,1,0:T(8,128)} custom-call(f32[32,16,32]{2,1,0:T(8,128)} %bitcast.9, f32[32]{0:T(128)} %sx_ref.1, f32[1,64]{1,0:T(1,128)} %bitcast.10, f32[1,64]{1,0:T(1,128)} %bitcast.11, bf16[2,256,256]{2,1,0:T(8,128)(2,1)} %constant.8.clone.wx_ref, bf16[2,256,256]{2,1,0:T(8,128)(2,1)} %constant.9.clone.wxt_ref, ...), custom_call_target="tpu_custom_call" | custom-call | tf_op jit(solution)/shard_map/pallas_call | solution.py:233
  18.2 1.7 %copy.10 = f32[2,32,16,16]{1,3,2,0:T(8,128)} copy(f32[2,32,16,16]{1,3,2,0:T(8,128)} %bitcast.8) | data formatting | bytes 131072

commit v2 on v1

--- a/solution.py
+++ b/solution.py
@@ -11,6 +11,7 @@
 MESH = pl.DeviceIdType.MESH
 LANES = 128
 ROWS = 8
+VMEM_BYTES = 16 * 2**20
 
 
 def mode_table(count):
@@ -62,8 +63,9 @@
 
 
 def kernel(
-    sizes, x_ref, sx_ref, sy_ref, sz_ref, wx_ref, wxt_ref, wy_ref, hz_ref, out_ref,
-    send, recv, send_back, recv_back, send_sem, recv_sem, send_back_sem, recv_back_sem,
+    sizes, x_hbm, sx_ref, sy_hbm, sz_hbm, wx_hbm, wy_hbm, hz_hbm, recv_back,
+    x_ref, sy_ref, sz_ref, wx_ref, wy_ref, hz_ref, send, recv, send_back,
+    load_sem, send_sem, recv_sem, send_back_sem, recv_back_sem,
 ):
     fields, count_x, rows_n, cols_n, share_y, share_z, planes = sizes
     devices = rows_n * cols_n
@@ -78,6 +80,22 @@
     for step in range(1, devices):
         peer = lax.rem(me + step, devices)
         pl.semaphore_signal(barrier, inc=1, device_id=place(peer), device_id_type=MESH)
+
+    loads = [
+        pltpu.make_async_copy(source, target, load_sem.at[i])
+        for i, (source, target) in enumerate(
+            [
+                (x_hbm, x_ref),
+                (wx_hbm, wx_ref),
+                (sy_hbm, sy_ref),
+                (sz_hbm, sz_ref),
+                (wy_hbm, wy_ref),
+                (hz_hbm, hz_ref),
+            ]
+        )
+    ]
+    for load in loads:
+        load.start()
 
     def exchange(source, target, source_sem, target_sem):
         copies = []
@@ -108,6 +126,8 @@
                 device_id_type=MESH,
             ).wait_recv()
 
+    loads[0].wait()
+    loads[1].wait()
     packed = jnp.concatenate(
         [
             jnp.concatenate([x_ref[f * share_y + h * ROWS + y] for y in range(ROWS)], axis=1)
@@ -133,6 +153,8 @@
     pl.semaphore_wait(barrier, devices - 1)
     copies = exchange(send, recv, send_sem, recv_sem)
 
+    for load in loads[2:]:
+        load.wait()
     count_z, count_y = sz_ref.shape[1], sy_ref.shape[1]
     width = rows_n * high_y * planes * ROWS
 
@@ -187,12 +209,20 @@
     for copy in copies:
         copy.wait_send()
     arrive(back_copies, send_back, recv_back, recv_back_sem)
-
+    for copy in back_copies:
+        copy.wait_send()
+
+
+def finish(sizes, tiles_ref, wxt_ref, out_ref):
+    fields, count_x, rows_n, cols_n, share_y, share_z, planes = sizes
+    high_y, high_z = share_y // ROWS, share_z // ROWS
+    groups = count_x // planes
     lane_tiles = count_x * ROWS // LANES
+    per_tile = groups // lane_tiles
     grid = [[None] * lane_tiles for _ in range(fields * high_y * high_z)]
     for f in range(fields):
         for t in range(lane_tiles):
-            tiles = [recv_back[f * groups + t * per_tile + i] for i in range(per_tile)]
+            tiles = [tiles_ref[f * groups + t * per_tile + i] for i in range(per_tile)]
             for i, tile in enumerate(swap_blocks(tiles)):
                 z, h = divmod(i, high_y)
                 grid[(f * high_y + h) * high_z + z][t] = tile
@@ -205,8 +235,6 @@
                 out_ref[f * share_y + h * ROWS + y] = values[
                     row : row + share_z, y * count_x : (y + 1) * count_x
                 ]
-    for copy in back_copies:
-        copy.wait_send()
 
 
 def fused(sizes, tracer, symbol_x, symbol_y, symbol_z):
@@ -227,26 +255,40 @@
     table_z = np.concatenate([high, low, high], axis=1)
 
     values = jnp.transpose(tracer, (0, 2, 3, 1)).reshape(fields * share_y, share_z, count_x)
+    hbm = pl.BlockSpec(memory_space=pltpu.HBM)
     vmem = pl.BlockSpec(memory_space=pltpu.VMEM)
     smem = pl.BlockSpec(memory_space=pltpu.SMEM)
-    tile = pltpu.VMEM((devices, ROWS, LANES), jnp.float32)
-    out = pl.pallas_call(
-        functools.partial(kernel, sizes),
-        out_shape=jax.ShapeDtypeStruct(values.shape, jnp.float32),
-        in_specs=[vmem, smem] + [vmem] * 6,
-        out_specs=vmem,
-        scratch_shapes=[tile] * 4 + [pltpu.SemaphoreType.DMA((devices,))] * 4,
-        compiler_params=pltpu.CompilerParams(collective_id=0, has_side_effects=True),
-    )(
+    tiles = jax.ShapeDtypeStruct((devices, ROWS, LANES), jnp.float32)
+    operands = (
         values,
         symbol_x,
         symbol_y.reshape(1, -1),
         symbol_z.reshape(1, -1),
         jnp.asarray(two_parts(table_x)),
-        jnp.asarray(two_parts(table_x.T)),
         jnp.asarray(two_parts(table_y)),
         jnp.asarray(table_z),
     )
+    held = [pltpu.VMEM(o.shape, o.dtype) for i, o in enumerate(operands) if i != 1]
+    back = pl.pallas_call(
+        functools.partial(kernel, sizes),
+        out_shape=tiles,
+        in_specs=[hbm, smem] + [hbm] * 5,
+        out_specs=vmem,
+        scratch_shapes=held
+        + [pltpu.VMEM(tiles.shape, tiles.dtype)] * 3
+        + [pltpu.SemaphoreType.DMA((len(held),))]
+        + [pltpu.SemaphoreType.DMA((devices,))] * 4,
+        compiler_params=pltpu.CompilerParams(
+            collective_id=0, has_side_effects=True, vmem_limit_bytes=VMEM_BYTES
+        ),
+    )(*operands)
+    out = pl.pallas_call(
+        functools.partial(finish, sizes),
+        out_shape=jax.ShapeDtypeStruct(values.shape, jnp.float32),
+        in_specs=[vmem, vmem],
+        out_specs=vmem,
+        compiler_params=pltpu.CompilerParams(vmem_limit_bytes=VMEM_BYTES),
+    )(back, jnp.asarray(two_parts(table_x.T)))
     out = out.reshape(fields, share_y, share_z, count_x)
     return jnp.transpose(out, (0, 3, 1, 2))
 

time: 20 us -> 22.2 us (1.11)
  local copies, waits for them, and re-layouts: 1.67 us -> 4.29 us
  Pallas kernels: 18.2 us -> 17.6 us
    unnamed x1 -> x16, local copies, waits for them, and re-layouts: 1.67 us -> 4.29 us
    pallas_call x1 -> x2, Pallas kernels: 18.2 us -> 17.6 us  [the longest x1 16.5 us: fused(): pl.pallas_call(functools.partial(kernel, sizes), out_shape=tiles, in_spec...]
where the time goes in v2:
time: 22.2 us; the launch traced here: 21.9 us
  Pallas kernels  17.6 us (79%)
  local copies, waits for them, and re-layouts  4.29 us (19%)
    pallas_call x1, Pallas kernels, fused(): pl.pallas_call(functools.partial(kernel, sizes), out_shape=tiles, in_spec...  16.5 us
    unnamed x16, local copies, waits for them, and re-layouts  4.29 us
    pallas_call x1, Pallas kernels, fused(): pl.pallas_call(functools.partial(finish, sizes), out_shape=jax.ShapeDtype...  1.06 us

profile of v2, /device:TPU:0, one launch (start us, length us, event | category | flops | bytes accessed | tf_op | source)
XLA Modules:
  0.0 21.9 jit_solution(13300855630213222822)
XLA Ops:
  0.0 0.0 copy-start.5
  0.0 0.0 copy-start.6
  0.0 0.0 copy-start.7
  0.0 0.6 %copy-done.5 = f32[32]{0:T(128)S(1)} copy-done((f32[32]{0:T(128)S(1)}, f32[32]{0:T(128)}, u32[]{:S(2)}) %copy-start.5) | copy-done | bytes 152
  0.7 0.0 copy-done.6
  0.7 0.0 copy-done.7
  0.7 0.0 copy-start.1
  0.7 0.9 %copy-done.1 = f32[2,32,16,16]{1,3,2,0:T(8,128)S(1)} copy-done((f32[2,32,16,16]{1,3,2,0:T(8,128)S(1)}, f32[2,32,16,16]{1,3,2,0:T(8,128)}, u32[]{:S(2)}) %copy-start.1) | copy-done | bytes 65560
  1.6 0.0 copy-start.2
  1.6 0.9 %copy-done.2 = bf16[2,256,256]{2,1,0:T(8,128)(2,1)S(1)} copy-done((bf16[2,256,256]{2,1,0:T(8,128)(2,1)S(1)}, bf16[2,256,256]{2,1,0:T(8,128)(2,1)}, u32[]{:S(2)}) %copy-start.2) | copy-done | bytes 262168
  2.6 0.0 copy-start.3
  2.6 0.9 %copy-done.3 = bf16[2,256,256]{2,1,0:T(8,128)(2,1)S(1)} copy-done((bf16[2,256,256]{2,1,0:T(8,128)(2,1)S(1)}, bf16[2,256,256]{2,1,0:T(8,128)(2,1)}, u32[]{:S(2)}) %copy-start.3) | copy-done | bytes 262168
  3.5 0.0 copy-start.4
  3.5 0.8 %copy-done.4 = bf16[64,192]{1,0:T(8,128)(2,1)S(1)} copy-done((bf16[64,192]{1,0:T(8,128)(2,1)S(1)}, bf16[64,192]{1,0:T(8,128)(2,1)}, u32[]{:S(2)}) %copy-start.4) | copy-done | bytes 24600
  4.3 0.0 copy-start
  4.3 16.5 %shard_map.82.tiles_ref = f32[16,8,128]{2,1,0:T(8,128)S(1)} custom-call(f32[32,16,32]{2,1,0:T(8,128)S(1)} %bitcast.8, f32[32]{0:T(128)S(1)} %copy-done.5, f32[1,64]{1,0:T(1,128)S(1)} %bitcast.9, f32[1,64]{1,0:T(1,128)S(1)} %bitcast.10, bf16[2,256,256]{2,1,0:T(8,128)(2,1)S(1)} %copy-done.3, bf16[2,256,256]{2,1,0:T(8,128)(2,1)S(1)} %copy-done.2, ...), custom_call_target="tpu_custom_call" | custom-call | tf_op jit(solution)/shard_map/pallas_call | solution.py:272
  20.8 0.0 copy-done
  20.8 1.1 %shard_map.83 = f32[32,16,32]{2,1,0:T(8,128)} custom-call(f32[16,8,128]{2,1,0:T(8,128)S(1)} %shard_map.82.tiles_ref, bf16[2,256,256]{2,1,0:T(8,128)(2,1)S(1)} %copy-done), custom_call_target="tpu_custom_call" | custom-call | tf_op jit(solution)/shard_map/pallas_call | solution.py:285
Async XLA Ops:
  0.0 0.7 %copy-start.5 = (f32[32]{0:T(128)S(1)}, f32[32]{0:T(128)}, u32[]{:S(2)}) copy-start(f32[32]{0:T(128)} %sx_ref.1) | copy-start | bytes 388
  0.0 0.7 %copy-start.6 = (f32[64]{0:T(128)S(1)}, f32[64]{0:T(128)}, u32[]{:S(2)}) copy-start(f32[64]{0:T(128)} %param.10) | copy-start | bytes 772
  0.0 0.7 %copy-start.7 = (f32[64]{0:T(128)S(1)}, f32[64]{0:T(128)}, u32[]{:S(2)}) copy-start(f32[64]{0:T(128)} %param.11) | copy-start | bytes 772
  0.7 0.9 %copy-start.1 = (f32[2,32,16,16]{1,3,2,0:T(8,128)S(1)}, f32[2,32,16,16]{1,3,2,0:T(8,128)}, u32[]{:S(2)}) copy-start(f32[2,32,16,16]{1,3,2,0:T(8,128)} %param.8) | copy-start | bytes 196612
  1.6 0.9 %copy-start.2 = (bf16[2,256,256]{2,1,0:T(8,128)(2,1)S(1)}, bf16[2,256,256]{2,1,0:T(8,128)(2,1)}, u32[]{:S(2)}) copy-start(bf16[2,256,256]{2,1,0:T(8,128)(2,1)} %constant.9.clone.wy_hbm) | copy-start | bytes 786436
  2.6 0.9 %copy-start.3 = (bf16[2,256,256]{2,1,0:T(8,128)(2,1)S(1)}, bf16[2,256,256]{2,1,0:T(8,128)(2,1)}, u32[]{:S(2)}) copy-start(bf16[2,256,256]{2,1,0:T(8,128)(2,1)} %constant.8.clone.wx_hbm) | copy-start | bytes 786436
  3.5 0.8 %copy-start.4 = (bf16[64,192]{1,0:T(8,128)(2,1)S(1)}, bf16[64,192]{1,0:T(8,128)(2,1)}, u32[]{:S(2)}) copy-start(bf16[64,192]{1,0:T(8,128)(2,1)} %constant.10.clone.hz_hbm) | copy-start | bytes 73732
  4.3 16.5 %copy-start = (bf16[2,256,256]{2,1,0:T(8,128)(2,1)S(1)}, bf16[2,256,256]{2,1,0:T(8,128)(2,1)}, u32[]{:S(2)}) copy-start(bf16[2,256,256]{2,1,0:T(8,128)(2,1)} %constant.11.clone.wxt_ref) | copy-start | bytes 786436

commit v3 on v2

--- a/solution.py
+++ b/solution.py
@@ -11,7 +11,6 @@
 MESH = pl.DeviceIdType.MESH
 LANES = 128
 ROWS = 8
-VMEM_BYTES = 16 * 2**20
 
 
 def mode_table(count):
@@ -279,7 +278,7 @@
         + [pltpu.SemaphoreType.DMA((len(held),))]
         + [pltpu.SemaphoreType.DMA((devices,))] * 4,
         compiler_params=pltpu.CompilerParams(
-            collective_id=0, has_side_effects=True, vmem_limit_bytes=VMEM_BYTES
+            collective_id=0, has_side_effects=True
         ),
     )(*operands)
     out = pl.pallas_call(
@@ -287,7 +286,7 @@
         out_shape=jax.ShapeDtypeStruct(values.shape, jnp.float32),
         in_specs=[vmem, vmem],
         out_specs=vmem,
-        compiler_params=pltpu.CompilerParams(vmem_limit_bytes=VMEM_BYTES),
+        compiler_params=pltpu.CompilerParams(),
     )(back, jnp.asarray(two_parts(table_x.T)))
     out = out.reshape(fields, share_y, share_z, count_x)
     return jnp.transpose(out, (0, 3, 1, 2))

time: 22.2 us -> 19.5 us (0.88)
  local copies, waits for them, and re-layouts: 4.29 us -> 0 us
  Pallas kernels: 17.6 us -> 19.3 us
    unnamed x16 -> x0, local copies, waits for them, and re-layouts: 4.29 us -> none
    pallas_call x1, Pallas kernels: 1.06 us -> 2.05 us  [fused(): pl.pallas_call(functools.partial(finish, sizes), out_shape=jax.ShapeDtype...]
    pallas_call x1, Pallas kernels: 16.5 us -> 17.2 us  [fused(): pl.pallas_call(functools.partial(kernel, sizes), out_shape=tiles, in_spec...]
where the time goes in v3:
time: 19.5 us; the launch traced here: 19.3 us
  Pallas kernels  19.3 us (99%)
    pallas_call x1, Pallas kernels, fused(): pl.pallas_call(functools.partial(kernel, sizes), out_shape=tiles, in_spec...  17.2 us
    pallas_call x1, Pallas kernels, fused(): pl.pallas_call(functools.partial(finish, sizes), out_shape=jax.ShapeDtype...  2.05 us

profile of v3, /device:TPU:0, one launch (start us, length us, event | category | flops | bytes accessed | tf_op | source)
XLA Modules:
  0.0 19.3 jit_solution(15315510900424099334)
XLA Ops:
  0.0 17.2 %shard_map.82.tiles_ref = f32[16,8,128]{2,1,0:T(8,128)} custom-call(f32[32,16,32]{2,1,0:T(8,128)} %bitcast.8, f32[32]{0:T(128)} %sx_ref.1, f32[1,64]{1,0:T(1,128)} %bitcast.9, f32[1,64]{1,0:T(1,128)} %bitcast.10, bf16[2,256,256]{2,1,0:T(8,128)(2,1)} %constant.8.clone.wx_hbm, bf16[2,256,256]{2,1,0:T(8,128)(2,1)} %constant.9.clone.wy_hbm, ...), custom_call_target="tpu_custom_call" | custom-call | tf_op jit(solution)/shard_map/pallas_call | solution.py:271
  17.2 2.1 %shard_map.83 = f32[32,16,32]{2,1,0:T(8,128)} custom-call(f32[16,8,128]{2,1,0:T(8,128)} %shard_map.82.tiles_ref, bf16[2,256,256]{2,1,0:T(8,128)(2,1)} %constant.11.clone.wxt_ref), custom_call_target="tpu_custom_call" | custom-call | tf_op jit(solution)/shard_map/pallas_call | solution.py:284
